TPU v7x, 128 devices: a whole 4x4x4 slice. The times are simulated.
128 devices in a mesh: asset: 32 (over y, z, core), tm: 4 (over x).
Axes of the slice: x: 4, y: 4, z: 4, core: 2. Of those that a mesh axis runs over, the one named last changes fastest.
Arguments:
- values: float32 [4, 1024, 65536], P(None, 'tm', 'asset'), may hold values from -64 to 64
- listed_from: int32 [65536], P('asset'), may hold values from -1024 to 1023, as said below
- listed_until: int32 [65536], P('asset'), may hold values from -960 to 3070, as said below
Outputs:
- standardized: float32 [4, 1024, 65536], P(None, 'tm', 'asset')
Inputs may be any that keep to these rules, and one draw needn't show every extreme that they name: listed_until[a] - listed_from[a] is at least 64. listed_until[a] - listed_from[a] is at least 64.
All inputs are finite; a program needn't handle non-finite values.
Results may differ from a plain program's by a relative error of at most 0.00005.
Values sent between devices are 32-bit elements; how exact they have to be, the bound alone decides.
A program may use at most 128 MiB of HBM per device.

v0:
```python
import functools

import jax
import jax.numpy as jnp
from jax import lax
from jax.experimental import pallas as pl
from jax.experimental.pallas import tpu as pltpu
from jax.sharding import PartitionSpec as P

WINDOW = 64
LANES = 128
CLIP = 3.0
UNROLL = 4


def field_groups(fields):
    half = (fields + 1) // 2
    return [(start, min(half, fields - start)) for start in range(0, fields, half)]


def kernel(
    n_tm, n_as, values, opened_hbm, closed_hbm, out,
    x, rolling, weight, inverse, opened_ref, closed_ref, part, got, totals,
    load_sem, halo_send, halo_recv, send_sem, recv_sem,
):
    fields, rows, assets = values.shape
    blocks = rows // WINDOW
    chunks = assets // LANES
    groups = field_groups(fields)
    tm = lax.axis_index("tm")
    me = lax.axis_index("asset")
    later = lax.rem(tm + 1, n_tm)
    before = lax.rem(tm + n_tm - 1, n_tm)

    dates = [
        pltpu.make_async_copy(opened_hbm, opened_ref, load_sem.at[fields]),
        pltpu.make_async_copy(closed_hbm, closed_ref, load_sem.at[fields + 1]),
    ]
    loads = [
        pltpu.make_async_copy(values.at[f], x.at[f, pl.ds(WINDOW, rows)], load_sem.at[f])
        for f in range(fields)
    ]

    barrier = pltpu.get_barrier_semaphore()
    for other in (later, before):
        pl.semaphore_signal(barrier, inc=1, device_id={"tm": other})
    for d in range(1, n_as):
        pl.semaphore_signal(barrier, inc=1, device_id={"asset": lax.rem(me + d, n_as)})
    for copy in dates + loads:
        copy.start()
    pl.semaphore_wait(barrier, n_as + 1)

    halos = [
        pltpu.make_async_remote_copy(
            src_ref=values.at[f, pl.ds(rows - WINDOW, WINDOW)],
            dst_ref=x.at[f, pl.ds(0, WINDOW)],
            send_sem=halo_send.at[f],
            recv_sem=halo_recv.at[f],
            device_id={"tm": later},
        )
        for f in range(fields)
    ]
    for copy in halos:
        copy.start()

    def send(slot):
        for d in range(1, n_as):
            pltpu.make_async_remote_copy(
                src_ref=part.at[slot],
                dst_ref=got.at[slot, d - 1],
                send_sem=send_sem.at[slot],
                recv_sem=recv_sem.at[slot],
                device_id={"asset": lax.rem(me + d, n_as)},
            ).start()

    def receive(slot):
        arrived = got.at[slot]
        pltpu.make_async_copy(arrived, arrived, recv_sem.at[slot]).wait()
        return part[slot] + jnp.sum(got[slot], axis=0)

    def row_of(first, second):
        return jnp.sum(jnp.concatenate([first, second], axis=0).T, axis=0, keepdims=True)

    def factors(row, count):
        mean = row / jnp.maximum(count, 1.0)
        other = pltpu.roll(mean, WINDOW, 1)
        scale = 1.0 / jnp.sqrt(jnp.maximum(mean - other * other, 0.0) + 0.1)
        lane = lax.broadcasted_iota(jnp.int32, row.shape, 1)
        both = jnp.broadcast_to(jnp.where(lane < WINDOW, mean, scale), (LANES, LANES)).T
        return both[:WINDOW], both[WINDOW:]

    def columns(c):
        return pl.ds(pl.multiple_of(c * LANES, LANES), LANES)

    zero = jnp.zeros((WINDOW, LANES), jnp.float32)
    part[...] = jnp.zeros(part.shape, part.dtype)
    first_stamp = tm * rows - WINDOW
    for copy in dates:
        copy.wait()

    @pl.loop(0, blocks + 1)
    def listing(b):
        start = pl.multiple_of(b * WINDOW, WINDOW)
        stamps = first_stamp + start + lax.broadcasted_iota(jnp.int32, (WINDOW, LANES), 0)

        def chunk(c, total):
            cols = columns(c)
            opened = jnp.maximum(opened_ref[:, cols], 0)
            closed = closed_ref[:, cols]
            listed = (stamps >= opened) & (stamps < closed)
            low = jnp.maximum(stamps - (WINDOW - 1), opened)
            counted = jnp.maximum(jnp.minimum(stamps + 1, closed) - low, 1).astype(jnp.float32)
            ones = jnp.where(listed, 1.0, 0.0)
            weight[pl.ds(start, WINDOW), cols] = ones
            inverse[pl.ds(start, WINDOW), cols] = ones / counted
            return total + ones

        total = lax.fori_loop(0, chunks, chunk, zero, unroll=2)
        part[0, pl.ds(lax.rem(b + blocks, blocks + 1), 1), :] = row_of(total, total)

    send(0)

    def roll_window(f, b):
        top = pl.multiple_of(b * WINDOW, WINDOW)

        def chunk(c, carry):
            cols = columns(c)
            reach = pl.ds(top, 2 * WINDOW)
            sums = x[f, reach, cols] * weight[reach, cols]
            for step in (8, 16, 32):
                sums = sums[step:] + sums[:-step]
            for step in (1, 2, 4):
                sums = sums + pltpu.roll(sums, step, 0)
            means = sums[8:] * inverse[pl.ds(top + WINDOW, WINDOW), cols]
            rolling[f, pl.ds(top, WINDOW), cols] = means
            return carry[0] + means, carry[1] + means * means

        return row_of(*lax.fori_loop(0, chunks, chunk, (zero, zero), unroll=UNROLL))

    def clip_scores(f, b, center, scale):
        top = pl.multiple_of(b * WINDOW, WINDOW)

        def chunk(c, carry):
            cols = columns(c)
            scored = (rolling[f, pl.ds(top, WINDOW), cols] - center) * scale
            clipped = jnp.minimum(jnp.maximum(scored, -CLIP), CLIP)
            masked = clipped * weight[pl.ds(top + WINDOW, WINDOW), cols]
            return carry[0] + masked, carry[1] + masked * clipped

        return row_of(*lax.fori_loop(0, chunks, chunk, (zero, zero), unroll=UNROLL))

    def finish(f, b, first, second):
        top = pl.multiple_of(b * WINDOW, WINDOW)
        center, scale = first
        middle, factor = second

        @pl.loop(0, chunks, unroll=UNROLL)
        def chunk(c):
            cols = columns(c)
            here = pl.ds(top, WINDOW)
            scored = (rolling[f, here, cols] - center) * scale
            clipped = jnp.minimum(jnp.maximum(scored, -CLIP), CLIP)
            deviate = (clipped - middle) * weight[pl.ds(top + WINDOW, WINDOW), cols]
            out[f, here, cols] = deviate * factor

    def count_row(b):
        return totals[0, pl.ds(b, 1), :]

    def total_row(slot, i):
        return totals[slot, pl.ds(i, 1), :]

    def main_first(g):
        start, size = groups[g]
        for f in range(start, start + size):
            loads[f].wait()

        @pl.loop(0, size * (blocks - 1))
        def item(i):
            f, b = start + lax.rem(i, size), 1 + lax.div(i, size)
            part[1 + 2 * g, pl.ds(i, 1), :] = roll_window(f, b)

        send(1 + 2 * g)

    def main_second(g):
        start, size = groups[g]
        slot = 1 + 2 * g
        totals[slot] = receive(slot)

        @pl.loop(0, size * (blocks - 1))
        def item(i):
            f, b = start + lax.rem(i, size), 1 + lax.div(i, size)
            center, scale = factors(total_row(slot, i), count_row(b))
            part[slot + 1, pl.ds(i, 1), :] = clip_scores(f, b, center, scale)

        send(slot + 1)

    def main_third(g):
        start, size = groups[g]
        slot = 1 + 2 * g
        totals[slot + 1] = receive(slot + 1)

        @pl.loop(0, size * (blocks - 1))
        def item(i):
            f, b = start + lax.rem(i, size), 1 + lax.div(i, size)
            count = count_row(b)
            first = factors(total_row(slot, i), count)
            finish(f, b, first, factors(total_row(slot + 1, i), count))

    tail_slot = 1 + 2 * len(groups)

    def tail_first(f):
        slot = tail_slot + 2 * f
        halos[f].wait_recv()
        part[slot, :1, :] = roll_window(f, 0)
        send(slot)

    def tail_second(f):
        slot = tail_slot + 2 * f
        totals[slot] = receive(slot)
        center, scale = factors(total_row(slot, 0), count_row(0))
        part[slot + 1, :1, :] = clip_scores(f, 0, center, scale)
        send(slot + 1)

    def tail_third(f):
        slot = tail_slot + 2 * f
        totals[slot + 1] = receive(slot + 1)
        first = factors(total_row(slot, 0), count_row(0))
        finish(f, 0, first, factors(total_row(slot + 1, 0), count_row(0)))

    early = min(2, fields)
    for g in range(len(groups)):
        main_first(g)
    totals[0] = receive(0)
    for step in range(max(early, len(groups))):
        if step < early:
            tail_first(step)
        if step < len(groups):
            main_second(step)
    for step in range(max(early, len(groups))):
        if step < early:
            tail_second(step)
        if step < len(groups):
            main_third(step)
    for f in range(early, fields):
        tail_first(f)
        if f > early:
            tail_second(f - 1)
        tail_third(f - early)
    if fields > early:
        tail_second(fields - 1)
    for f in range(fields - early, fields):
        tail_third(f)

    for copy in halos:
        copy.wait_send()
    for slot in range(part.shape[0]):
        sent = got.at[slot]
        pltpu.make_async_copy(sent, sent, send_sem.at[slot]).wait()


def per_device(n_tm, n_as, values, listed_from, listed_until):
    fields, rows, assets = values.shape
    blocks = rows // WINDOW
    groups = field_groups(fields)
    stats = -(-max(groups[0][1] * (blocks - 1), blocks + 1) // 8) * 8
    slots = 1 + 2 * len(groups) + 2 * fields
    f32 = jnp.float32
    vmem = pltpu.VMEM
    dma = pltpu.SemaphoreType.DMA
    return pl.pallas_call(
        functools.partial(kernel, n_tm, n_as),
        out_shape=vmem((fields, rows, assets), f32),
        in_specs=[pl.BlockSpec(memory_space=pltpu.HBM)] * 3,
        out_specs=pl.BlockSpec(memory_space=vmem),
        scratch_shapes=[
            vmem((fields, WINDOW + rows, assets), f32),
            vmem((fields, rows, assets), f32),
            vmem((WINDOW + rows, assets), f32),
            vmem((WINDOW + rows, assets), f32),
            vmem((1, assets), jnp.int32),
            vmem((1, assets), jnp.int32),
            vmem((slots, stats, LANES), f32),
            vmem((slots, n_as - 1, stats, LANES), f32),
            vmem((slots, stats, LANES), f32),
            dma((fields + 2,)),
            dma((fields,)),
            dma((fields,)),
            dma((slots,)),
            dma((slots,)),
        ],
        compiler_params=pltpu.CompilerParams(
            collective_id=0, has_side_effects=True, vmem_limit_bytes=48 * 2**20
        ),
    )(values, listed_from[None], listed_until[None])


def solution(mesh):
    in_specs = (P(None, "tm", "asset"), P("asset"), P("asset"))
    out_specs = P(None, "tm", "asset")
    body = functools.partial(per_device, mesh.shape["tm"], mesh.shape["asset"])
    return jax.shard_map(
        body, mesh=mesh, in_specs=in_specs, out_specs=out_specs, check_vma=False
    )
```

profile of v0, /device:TPU:1, one launch (start us, length us, event | category | flops | bytes accessed | tf_op | source)
XLA Modules:
  0.0 72.5 jit_solution(18112648493715771731)
XLA Ops:
  0.0 69.1 %shard_map.37 = f32[4,256,2048]{2,1,0:T(8,128)S(1)} custom-call(f32[4,256,2048]{2,1,0:T(8,128)} %values.1, s32[1,2048]{1,0:T(1,128)} %bitcast.2, s32[1,2048]{1,0:T(1,128)} %bitcast.3), custom_call_target="tpu_custom_call" | custom-call | tf_op jit(solution)/shard_map/pallas_call | solution.py:270
  69.1 3.4 %copy.5 = f32[4,256,2048]{2,1,0:T(8,128)} copy(f32[4,256,2048]{2,1,0:T(8,128)S(1)} %shard_map.37) | data formatting | bytes 16777216
where the time goes:
time: 72.6 us; the launch traced here: 72.5 us
  Pallas kernels  69.1 us (95%)
  local copies, waits for them, and re-layouts  3.4 us (5%)
    pallas_call x1, Pallas kernels, per_device(): pl.pallas_call(functools.partial(kernel, n_tm, n_as), out_shape=vmem((fie...  69.1 us
    unnamed x1, local copies, waits for them, and re-layouts  3.4 us

commit v1 on v0

--- a/solution.py
+++ b/solution.py
@@ -11,6 +11,7 @@
 LANES = 128
 CLIP = 3.0
 UNROLL = 4
+LINE = 8
 
 
 def field_groups(fields):
@@ -20,17 +21,25 @@
 
 def kernel(
     n_tm, n_as, values, opened_hbm, closed_hbm, out,
-    x, rolling, weight, inverse, opened_ref, closed_ref, part, got, totals,
-    load_sem, halo_send, halo_recv, send_sem, recv_sem,
+    x, rolling, weight, inverse, opened_ref, closed_ref, stage,
+    part, got, totals, tail_part, tail_got, tail_totals,
+    load_sem, halo_send, halo_recv, next_sem, done_sem, ready,
+    send_sem, recv_sem, tail_send, tail_recv,
 ):
     fields, rows, assets = values.shape
     blocks = rows // WINDOW
     chunks = assets // LANES
     groups = field_groups(fields)
+    ahead = fields - 1
     tm = lax.axis_index("tm")
     me = lax.axis_index("asset")
     later = lax.rem(tm + 1, n_tm)
     before = lax.rem(tm + n_tm - 1, n_tm)
+    is_first = tm == 0
+    is_last = tm == n_tm - 1
+    spot = lax.rem(me, LINE)
+    line_peers = [me - spot + lax.rem(spot + d, LINE) for d in range(1, LINE)]
+    cross_peers = [lax.rem(me + LINE * d, n_as) for d in range(1, n_as // LINE)]
 
     dates = [
         pltpu.make_async_copy(opened_hbm, opened_ref, load_sem.at[fields]),
@@ -44,11 +53,11 @@
     barrier = pltpu.get_barrier_semaphore()
     for other in (later, before):
         pl.semaphore_signal(barrier, inc=1, device_id={"tm": other})
-    for d in range(1, n_as):
-        pl.semaphore_signal(barrier, inc=1, device_id={"asset": lax.rem(me + d, n_as)})
+    for other in line_peers + cross_peers:
+        pl.semaphore_signal(barrier, inc=1, device_id={"asset": other})
     for copy in dates + loads:
         copy.start()
-    pl.semaphore_wait(barrier, n_as + 1)
+    pl.semaphore_wait(barrier, 2 + len(line_peers) + len(cross_peers))
 
     halos = [
         pltpu.make_async_remote_copy(
@@ -58,10 +67,27 @@
             recv_sem=halo_recv.at[f],
             device_id={"tm": later},
         )
-        for f in range(fields)
+        for f in range(fields - 1)
     ]
+    upcoming = pltpu.make_async_remote_copy(
+        src_ref=values.at[ahead, pl.ds(0, WINDOW)],
+        dst_ref=x.at[ahead, pl.ds(WINDOW + rows, WINDOW)],
+        send_sem=next_sem.at[0],
+        recv_sem=next_sem.at[1],
+        device_id={"tm": before},
+    )
+    finished = pltpu.make_async_remote_copy(
+        src_ref=stage,
+        dst_ref=out.at[ahead, pl.ds(0, WINDOW)],
+        send_sem=done_sem.at[0],
+        recv_sem=done_sem.at[1],
+        device_id={"tm": later},
+    )
+    pl.when(jnp.logical_not(is_first))(upcoming.start)
     for copy in halos:
         copy.start()
+    for other in cross_peers:
+        pl.semaphore_signal(ready, inc=1, device_id={"asset": other})
 
     def send(slot):
         for d in range(1, n_as):
@@ -78,6 +104,21 @@
         pltpu.make_async_copy(arrived, arrived, recv_sem.at[slot]).wait()
         return part[slot] + jnp.sum(got[slot], axis=0)
 
+    def send_row(slot):
+        for d in range(1, n_as):
+            pltpu.make_async_remote_copy(
+                src_ref=tail_part.at[slot],
+                dst_ref=tail_got.at[slot, pl.ds(d - 1, 1)],
+                send_sem=tail_send.at[slot],
+                recv_sem=tail_recv.at[slot],
+                device_id={"asset": lax.rem(me + d, n_as)},
+            ).start()
+
+    def receive_row(slot):
+        arrived = tail_got.at[slot]
+        pltpu.make_async_copy(arrived, arrived, tail_recv.at[slot]).wait()
+        tail_totals[slot] = tail_part[slot] + jnp.sum(tail_got[slot], axis=0, keepdims=True)
+
     def row_of(first, second):
         return jnp.sum(jnp.concatenate([first, second], axis=0).T, axis=0, keepdims=True)
 
@@ -94,11 +135,16 @@
 
     zero = jnp.zeros((WINDOW, LANES), jnp.float32)
     part[...] = jnp.zeros(part.shape, part.dtype)
+
+    @pl.when(is_first)
+    def no_past():
+        x[ahead, :WINDOW, :] = jnp.zeros((WINDOW, assets), jnp.float32)
+
     first_stamp = tm * rows - WINDOW
     for copy in dates:
         copy.wait()
 
-    @pl.loop(0, blocks + 1)
+    @pl.loop(0, blocks + 2)
     def listing(b):
         start = pl.multiple_of(b * WINDOW, WINDOW)
         stamps = first_stamp + start + lax.broadcasted_iota(jnp.int32, (WINDOW, LANES), 0)
@@ -116,8 +162,9 @@
             return total + ones
 
         total = lax.fori_loop(0, chunks, chunk, zero, unroll=2)
-        part[0, pl.ds(lax.rem(b + blocks, blocks + 1), 1), :] = row_of(total, total)
-
+        part[0, pl.ds(lax.rem(b + blocks + 1, blocks + 2), 1), :] = row_of(total, total)
+
+    pl.semaphore_wait(ready, len(cross_peers))
     send(0)
 
     def roll_window(f, b):
@@ -149,107 +196,139 @@
 
         return row_of(*lax.fori_loop(0, chunks, chunk, (zero, zero), unroll=UNROLL))
 
-    def finish(f, b, first, second):
+    def finish(f, b, first, second, target, base):
         top = pl.multiple_of(b * WINDOW, WINDOW)
+        base = pl.multiple_of(base, WINDOW)
         center, scale = first
         middle, factor = second
 
         @pl.loop(0, chunks, unroll=UNROLL)
         def chunk(c):
             cols = columns(c)
-            here = pl.ds(top, WINDOW)
-            scored = (rolling[f, here, cols] - center) * scale
+            scored = (rolling[f, pl.ds(top, WINDOW), cols] - center) * scale
             clipped = jnp.minimum(jnp.maximum(scored, -CLIP), CLIP)
             deviate = (clipped - middle) * weight[pl.ds(top + WINDOW, WINDOW), cols]
-            out[f, here, cols] = deviate * factor
+            target[pl.ds(base, WINDOW), cols] = deviate * factor
 
     def count_row(b):
         return totals[0, pl.ds(b, 1), :]
 
     def total_row(slot, i):
         return totals[slot, pl.ds(i, 1), :]
+
+    def items(g):
+        start, size = groups[g]
+        whole = size * (blocks - 1)
+        if start + size < fields:
+            return whole, lambda i: (start + lax.rem(i, size), 1 + lax.div(i, size))
+        return whole + is_first.astype(jnp.int32), lambda i: (
+            jnp.where(i < whole, start + lax.rem(i, size), ahead),
+            jnp.where(i < whole, 1 + lax.div(i, size), 0),
+        )
 
     def main_first(g):
         start, size = groups[g]
         for f in range(start, start + size):
             loads[f].wait()
-
-        @pl.loop(0, size * (blocks - 1))
+        number, place = items(g)
+
+        @pl.loop(0, number)
         def item(i):
-            f, b = start + lax.rem(i, size), 1 + lax.div(i, size)
+            f, b = place(i)
             part[1 + 2 * g, pl.ds(i, 1), :] = roll_window(f, b)
 
         send(1 + 2 * g)
 
     def main_second(g):
-        start, size = groups[g]
         slot = 1 + 2 * g
         totals[slot] = receive(slot)
-
-        @pl.loop(0, size * (blocks - 1))
+        number, place = items(g)
+
+        @pl.loop(0, number)
         def item(i):
-            f, b = start + lax.rem(i, size), 1 + lax.div(i, size)
+            f, b = place(i)
             center, scale = factors(total_row(slot, i), count_row(b))
             part[slot + 1, pl.ds(i, 1), :] = clip_scores(f, b, center, scale)
 
         send(slot + 1)
 
     def main_third(g):
-        start, size = groups[g]
         slot = 1 + 2 * g
         totals[slot + 1] = receive(slot + 1)
-
-        @pl.loop(0, size * (blocks - 1))
+        number, place = items(g)
+
+        @pl.loop(0, number)
         def item(i):
-            f, b = start + lax.rem(i, size), 1 + lax.div(i, size)
+            f, b = place(i)
             count = count_row(b)
             first = factors(total_row(slot, i), count)
-            finish(f, b, first, factors(total_row(slot + 1, i), count))
-
-    tail_slot = 1 + 2 * len(groups)
-
-    def tail_first(f):
-        slot = tail_slot + 2 * f
+            second = factors(total_row(slot + 1, i), count)
+            finish(f, b, first, second, out.at[f], b * WINDOW)
+
+    def tail_first(f, b):
+        tail_part[2 * f] = roll_window(f, b)
+        send_row(2 * f)
+
+    def tail_second(f, b):
+        slot = 2 * f
+        receive_row(slot)
+        center, scale = factors(tail_totals[slot], count_row(b))
+        tail_part[slot + 1] = clip_scores(f, b, center, scale)
+        send_row(slot + 1)
+
+    def tail_third(f, b, target):
+        slot = 2 * f
+        receive_row(slot + 1)
+        count = count_row(b)
+        first = factors(tail_totals[slot], count)
+        second = factors(tail_totals[slot + 1], count)
+        finish(f, b, first, second, target, 0)
+
+    def ahead_first():
+        upcoming.wait_recv()
+        tail_first(ahead, blocks)
+
+    def ahead_second():
+        tail_second(ahead, blocks)
+
+    def ahead_third():
+        tail_third(ahead, blocks, stage)
+        finished.start()
+
+    not_last = pl.when(jnp.logical_not(is_last))
+
+    def first(f):
         halos[f].wait_recv()
-        part[slot, :1, :] = roll_window(f, 0)
-        send(slot)
-
-    def tail_second(f):
-        slot = tail_slot + 2 * f
-        totals[slot] = receive(slot)
-        center, scale = factors(total_row(slot, 0), count_row(0))
-        part[slot + 1, :1, :] = clip_scores(f, 0, center, scale)
-        send(slot + 1)
-
-    def tail_third(f):
-        slot = tail_slot + 2 * f
-        totals[slot + 1] = receive(slot + 1)
-        first = factors(total_row(slot, 0), count_row(0))
-        finish(f, 0, first, factors(total_row(slot + 1, 0), count_row(0)))
-
-    early = min(2, fields)
-    for g in range(len(groups)):
-        main_first(g)
+        tail_first(f, 0)
+
+    def second(f):
+        tail_second(f, 0)
+
+    def third(f):
+        tail_third(f, 0, out.at[f])
+
+    main_first(0)
+    main_first(1)
     totals[0] = receive(0)
-    for step in range(max(early, len(groups))):
-        if step < early:
-            tail_first(step)
-        if step < len(groups):
-            main_second(step)
-    for step in range(max(early, len(groups))):
-        if step < early:
-            tail_second(step)
-        if step < len(groups):
-            main_third(step)
-    for f in range(early, fields):
-        tail_first(f)
-        if f > early:
-            tail_second(f - 1)
-        tail_third(f - early)
-    if fields > early:
-        tail_second(fields - 1)
-    for f in range(fields - early, fields):
-        tail_third(f)
+    main_second(0)
+    not_last(ahead_first)
+    main_second(1)
+    first(0)
+    not_last(ahead_second)
+    main_third(0)
+    second(0)
+    not_last(ahead_third)
+    main_third(1)
+    third(0)
+    for f in range(1, fields - 1):
+        first(f)
+        second(f)
+        third(f)
+
+    @pl.when(jnp.logical_not(is_first))
+    def arrivals():
+        finished.wait_recv()
+        upcoming.wait_send()
 
     for copy in halos:
         copy.wait_send()
@@ -257,13 +336,26 @@
         sent = got.at[slot]
         pltpu.make_async_copy(sent, sent, send_sem.at[slot]).wait()
 
+    def row_sent(slot):
+        sent = tail_got.at[slot]
+        pltpu.make_async_copy(sent, sent, tail_send.at[slot]).wait()
+
+    for slot in range(2 * ahead):
+        row_sent(slot)
+
+    @not_last
+    def departures():
+        finished.wait_send()
+        row_sent(2 * ahead)
+        row_sent(2 * ahead + 1)
+
 
 def per_device(n_tm, n_as, values, listed_from, listed_until):
     fields, rows, assets = values.shape
     blocks = rows // WINDOW
     groups = field_groups(fields)
-    stats = -(-max(groups[0][1] * (blocks - 1), blocks + 1) // 8) * 8
-    slots = 1 + 2 * len(groups) + 2 * fields
+    stats = -(-max(groups[0][1] * (blocks - 1) + 1, blocks + 2) // 8) * 8
+    slots = 1 + 2 * len(groups)
     f32 = jnp.float32
     vmem = pltpu.VMEM
     dma = pltpu.SemaphoreType.DMA
@@ -273,20 +365,29 @@
         in_specs=[pl.BlockSpec(memory_space=pltpu.HBM)] * 3,
         out_specs=pl.BlockSpec(memory_space=vmem),
         scratch_shapes=[
-            vmem((fields, WINDOW + rows, assets), f32),
-            vmem((fields, rows, assets), f32),
-            vmem((WINDOW + rows, assets), f32),
-            vmem((WINDOW + rows, assets), f32),
+            vmem((fields, rows + 2 * WINDOW, assets), f32),
+            vmem((fields, rows + WINDOW, assets), f32),
+            vmem((rows + 2 * WINDOW, assets), f32),
+            vmem((rows + 2 * WINDOW, assets), f32),
             vmem((1, assets), jnp.int32),
             vmem((1, assets), jnp.int32),
+            vmem((WINDOW, assets), f32),
             vmem((slots, stats, LANES), f32),
             vmem((slots, n_as - 1, stats, LANES), f32),
             vmem((slots, stats, LANES), f32),
+            vmem((2 * fields, 1, LANES), f32),
+            vmem((2 * fields, n_as - 1, LANES), f32),
+            vmem((2 * fields, 1, LANES), f32),
             dma((fields + 2,)),
             dma((fields,)),
             dma((fields,)),
+            dma((2,)),
+            dma((2,)),
+            pltpu.SemaphoreType.REGULAR,
             dma((slots,)),
             dma((slots,)),
+            dma((2 * fields,)),
+            dma((2 * fields,)),
         ],
         compiler_params=pltpu.CompilerParams(
             collective_id=0, has_side_effects=True, vmem_limit_bytes=48 * 2**20

time: 72.6 us -> 63.5 us (0.87)
  Pallas kernels: 69.1 us -> 59.9 us
    pallas_call x1, Pallas kernels: 69.1 us -> 59.9 us  [per_device(): pl.pallas_call(functools.partial(kernel, n_tm, n_as), out_shape=vmem((fie...]
where the time goes in v1:
time: 63.5 us; the launch traced here: 63.4 us
  Pallas kernels  59.9 us (94%)
  local copies, waits for them, and re-layouts  3.4 us (5%)
    pallas_call x1, Pallas kernels, per_device(): pl.pallas_call(functools.partial(kernel, n_tm, n_as), out_shape=vmem((fie...  59.9 us
    unnamed x1, local copies, waits for them, and re-layouts  3.4 us

profile of v1, /device:TPU:1, one launch (start us, length us, event | category | flops | bytes accessed | tf_op | source)
XLA Modules:
  0.0 63.4 jit_solution(7093955580573219174)
XLA Ops:
  0.0 59.9 %shard_map.37 = f32[4,256,2048]{2,1,0:T(8,128)S(1)} custom-call(f32[4,256,2048]{2,1,0:T(8,128)} %values.1, s32[1,2048]{1,0:T(1,128)} %bitcast.2, s32[1,2048]{1,0:T(1,128)} %bitcast.3), custom_call_target="tpu_custom_call" | custom-call | tf_op jit(solution)/shard_map/pallas_call | solution.py:362
  60.0 3.4 %copy.5 = f32[4,256,2048]{2,1,0:T(8,128)} copy(f32[4,256,2048]{2,1,0:T(8,128)S(1)} %shard_map.37) | data formatting | bytes 16777216

commit v2 on v1

--- a/solution.py
+++ b/solution.py
@@ -12,6 +12,7 @@
 CLIP = 3.0
 UNROLL = 4
 LINE = 8
+DIRECT = 1280
 
 
 def field_groups(fields):
@@ -21,9 +22,9 @@
 
 def kernel(
     n_tm, n_as, values, opened_hbm, closed_hbm, out,
-    x, rolling, weight, inverse, opened_ref, closed_ref, stage,
-    part, got, totals, tail_part, tail_got, tail_totals,
-    load_sem, halo_send, halo_recv, next_sem, done_sem, ready,
+    x, rolling, weight, inverse, opened_ref, closed_ref, stage, hold, lanes, spread,
+    part, got, totals, tail_part, tail_got,
+    load_sem, halo_send, halo_recv, next_sem, done_sem, hold_send, hold_recv, late_send, late_recv, ready,
     send_sem, recv_sem, tail_send, tail_recv,
 ):
     fields, rows, assets = values.shape
@@ -35,6 +36,7 @@
     me = lax.axis_index("asset")
     later = lax.rem(tm + 1, n_tm)
     before = lax.rem(tm + n_tm - 1, n_tm)
+    across = lax.rem(tm + 2, n_tm)
     is_first = tm == 0
     is_last = tm == n_tm - 1
     spot = lax.rem(me, LINE)
@@ -51,18 +53,60 @@
     ]
 
     barrier = pltpu.get_barrier_semaphore()
-    for other in (later, before):
+    for other in (later, before, across):
         pl.semaphore_signal(barrier, inc=1, device_id={"tm": other})
     for other in line_peers + cross_peers:
         pl.semaphore_signal(barrier, inc=1, device_id={"asset": other})
     for copy in dates + loads:
         copy.start()
-    pl.semaphore_wait(barrier, 2 + len(line_peers) + len(cross_peers))
-
+
+    def columns(c):
+        return pl.ds(pl.multiple_of(c * LANES, LANES), LANES)
+
+    zero = jnp.zeros((WINDOW, LANES), jnp.float32)
+    part[...] = jnp.zeros(part.shape, part.dtype)
+    lanes[...] = jnp.zeros(lanes.shape, lanes.dtype)
+
+    @pl.when(is_first)
+    def no_past():
+        x[ahead, :WINDOW, :] = jnp.zeros((WINDOW, assets), jnp.float32)
+        x[ahead - 1, :WINDOW, DIRECT:] = jnp.zeros((WINDOW, assets - DIRECT), jnp.float32)
+
+    first_stamp = tm * rows - WINDOW
+    for copy in dates:
+        copy.wait()
+
+    @pl.loop(0, blocks + 2)
+    def listing(b):
+        start = pl.multiple_of(b * WINDOW, WINDOW)
+        stamps = first_stamp + start + lax.broadcasted_iota(jnp.int32, (WINDOW, LANES), 0)
+
+        def chunk(c, total):
+            cols = columns(c)
+            opened = jnp.maximum(opened_ref[:, cols], 0)
+            closed = closed_ref[:, cols]
+            listed = (stamps >= opened) & (stamps < closed)
+            low = jnp.maximum(stamps - (WINDOW - 1), opened)
+            counted = jnp.maximum(jnp.minimum(stamps + 1, closed) - low, 1).astype(jnp.float32)
+            ones = jnp.where(listed, 1.0, 0.0)
+            weight[pl.ds(start, WINDOW), cols] = ones
+            inverse[pl.ds(start, WINDOW), cols] = ones / counted
+            return total + ones
+
+        total = lax.fori_loop(0, chunks, chunk, zero, unroll=2)
+        here = lax.rem(b + blocks + 1, blocks + 2)
+        lanes[0, here, :WINDOW] = total
+        lanes[0, here, WINDOW:] = total
+
+    pl.semaphore_wait(barrier, 3 + len(line_peers) + len(cross_peers))
+
+    past = pl.ds(rows - WINDOW, WINDOW)
+    direct = [pl.ds(0, assets if f < ahead - 1 else DIRECT) for f in range(ahead)]
+    rest = pl.ds(DIRECT, assets - DIRECT)
     halos = [
         pltpu.make_async_remote_copy(
-            src_ref=values.at[f, pl.ds(rows - WINDOW, WINDOW)],
-            dst_ref=x.at[f, pl.ds(0, WINDOW)],
+            src_ref=values.at[f, past, direct[f]],
+            dst_ref=x.at[f, pl.ds(0, WINDOW), direct[f]],
             send_sem=halo_send.at[f],
             recv_sem=halo_recv.at[f],
             device_id={"tm": later},
@@ -83,7 +127,32 @@
         recv_sem=done_sem.at[1],
         device_id={"tm": later},
     )
+
+    def detour(slot, other):
+        return pltpu.make_async_remote_copy(
+            src_ref=values.at[ahead - 1, past, rest],
+            dst_ref=hold.at[slot],
+            send_sem=hold_send.at[0],
+            recv_sem=hold_recv.at[slot],
+            device_id={"tm": other},
+        )
+
+    def onward(slot, other):
+        return pltpu.make_async_remote_copy(
+            src_ref=hold.at[slot],
+            dst_ref=x.at[ahead - 1, pl.ds(0, WINDOW), rest],
+            send_sem=late_send.at[slot],
+            recv_sem=late_recv.at[0],
+            device_id={"tm": other},
+        )
+
+    is_even = lax.rem(tm, 2) == 0
+    even_detour, odd_detour = detour(0, before), detour(1, across)
+    cross_onward, back_onward = onward(0, across), onward(1, before)
+
     pl.when(jnp.logical_not(is_first))(upcoming.start)
+    pl.when(is_even)(even_detour.start)
+    pl.when(tm == 1)(odd_detour.start)
     for copy in halos:
         copy.start()
     for other in cross_peers:
@@ -117,57 +186,23 @@
     def receive_row(slot):
         arrived = tail_got.at[slot]
         pltpu.make_async_copy(arrived, arrived, tail_recv.at[slot]).wait()
-        tail_totals[slot] = tail_part[slot] + jnp.sum(tail_got[slot], axis=0, keepdims=True)
-
-    def row_of(first, second):
-        return jnp.sum(jnp.concatenate([first, second], axis=0).T, axis=0, keepdims=True)
-
-    def factors(row, count):
+        return tail_part[slot] + jnp.sum(tail_got[slot], axis=0, keepdims=True)
+
+    def row_of(both):
+        return jnp.sum(both.T, axis=0, keepdims=True)
+
+    def factor_rows(row, count):
         mean = row / jnp.maximum(count, 1.0)
         other = pltpu.roll(mean, WINDOW, 1)
         scale = 1.0 / jnp.sqrt(jnp.maximum(mean - other * other, 0.0) + 0.1)
         lane = lax.broadcasted_iota(jnp.int32, row.shape, 1)
-        both = jnp.broadcast_to(jnp.where(lane < WINDOW, mean, scale), (LANES, LANES)).T
-        return both[:WINDOW], both[WINDOW:]
-
-    def columns(c):
-        return pl.ds(pl.multiple_of(c * LANES, LANES), LANES)
-
-    zero = jnp.zeros((WINDOW, LANES), jnp.float32)
-    part[...] = jnp.zeros(part.shape, part.dtype)
-
-    @pl.when(is_first)
-    def no_past():
-        x[ahead, :WINDOW, :] = jnp.zeros((WINDOW, assets), jnp.float32)
-
-    first_stamp = tm * rows - WINDOW
-    for copy in dates:
-        copy.wait()
-
-    @pl.loop(0, blocks + 2)
-    def listing(b):
-        start = pl.multiple_of(b * WINDOW, WINDOW)
-        stamps = first_stamp + start + lax.broadcasted_iota(jnp.int32, (WINDOW, LANES), 0)
-
-        def chunk(c, total):
-            cols = columns(c)
-            opened = jnp.maximum(opened_ref[:, cols], 0)
-            closed = closed_ref[:, cols]
-            listed = (stamps >= opened) & (stamps < closed)
-            low = jnp.maximum(stamps - (WINDOW - 1), opened)
-            counted = jnp.maximum(jnp.minimum(stamps + 1, closed) - low, 1).astype(jnp.float32)
-            ones = jnp.where(listed, 1.0, 0.0)
-            weight[pl.ds(start, WINDOW), cols] = ones
-            inverse[pl.ds(start, WINDOW), cols] = ones / counted
-            return total + ones
-
-        total = lax.fori_loop(0, chunks, chunk, zero, unroll=2)
-        part[0, pl.ds(lax.rem(b + blocks + 1, blocks + 2), 1), :] = row_of(total, total)
-
-    pl.semaphore_wait(ready, len(cross_peers))
-    send(0)
-
-    def roll_window(f, b):
+        return jnp.where(lane < WINDOW, mean, scale)
+
+    def upright(row):
+        return jnp.broadcast_to(row, (LANES, LANES)).T
+
+
+    def roll_window(f, b, place):
         top = pl.multiple_of(b * WINDOW, WINDOW)
 
         def chunk(c, carry):
@@ -182,39 +217,46 @@
             rolling[f, pl.ds(top, WINDOW), cols] = means
             return carry[0] + means, carry[1] + means * means
 
-        return row_of(*lax.fori_loop(0, chunks, chunk, (zero, zero), unroll=UNROLL))
-
-    def clip_scores(f, b, center, scale):
+        total, square = lax.fori_loop(0, chunks, chunk, (zero, zero), unroll=UNROLL)
+        place[:WINDOW] = total
+        place[WINDOW:] = square
+
+    def clip_scores(f, b, tall, place):
         top = pl.multiple_of(b * WINDOW, WINDOW)
+        center, scale = tall[:WINDOW], tall[WINDOW:]
 
         def chunk(c, carry):
             cols = columns(c)
-            scored = (rolling[f, pl.ds(top, WINDOW), cols] - center) * scale
+            here = pl.ds(top, WINDOW)
+            scored = (rolling[f, here, cols] - center) * scale
             clipped = jnp.minimum(jnp.maximum(scored, -CLIP), CLIP)
+            rolling[f, here, cols] = clipped
             masked = clipped * weight[pl.ds(top + WINDOW, WINDOW), cols]
             return carry[0] + masked, carry[1] + masked * clipped
 
-        return row_of(*lax.fori_loop(0, chunks, chunk, (zero, zero), unroll=UNROLL))
-
-    def finish(f, b, first, second, target, base):
+        total, square = lax.fori_loop(0, chunks, chunk, (zero, zero), unroll=UNROLL)
+        place[:WINDOW] = total
+        place[WINDOW:] = square
+
+    def finish(f, b, tall, target, base):
         top = pl.multiple_of(b * WINDOW, WINDOW)
         base = pl.multiple_of(base, WINDOW)
-        center, scale = first
-        middle, factor = second
+        middle, factor = tall[:WINDOW], tall[WINDOW:]
 
         @pl.loop(0, chunks, unroll=UNROLL)
         def chunk(c):
             cols = columns(c)
-            scored = (rolling[f, pl.ds(top, WINDOW), cols] - center) * scale
-            clipped = jnp.minimum(jnp.maximum(scored, -CLIP), CLIP)
+            clipped = rolling[f, pl.ds(top, WINDOW), cols]
             deviate = (clipped - middle) * weight[pl.ds(top + WINDOW, WINDOW), cols]
             target[pl.ds(base, WINDOW), cols] = deviate * factor
 
-    def count_row(b):
-        return totals[0, pl.ds(b, 1), :]
-
-    def total_row(slot, i):
-        return totals[slot, pl.ds(i, 1), :]
+    def places(g):
+        start, size = groups[g]
+        number = size * (blocks - 1)
+        where = [(start + i % size, 1 + i // size) for i in range(number)]
+        if start + size == fields:
+            where.append((ahead, 0))
+        return where
 
     def items(g):
         start, size = groups[g]
@@ -226,6 +268,25 @@
             jnp.where(i < whole, 1 + lax.div(i, size), 0),
         )
 
+    def gather_rows(g, slot):
+        for i in range(len(places(g))):
+            part[slot, pl.ds(i, 1), :] = row_of(lanes[1 + g, i])
+        send(slot)
+
+    def spread_rows(g, slot):
+        total = receive(slot)
+        number = len(places(g))
+        count = jnp.concatenate([totals[pl.ds(b, 1), :] for _, b in places(g)], axis=0)
+        rows_of = factor_rows(total[:number], count)
+        for i in range(number):
+            spread[g, i] = upright(rows_of[i : i + 1])
+
+    def meet_plane():
+        for i in range(blocks + 1):
+            part[0, pl.ds(i, 1), :] = row_of(lanes[0, i])
+        pl.semaphore_wait(ready, len(cross_peers))
+        send(0)
+
     def main_first(g):
         start, size = groups[g]
         for f in range(start, start + size):
@@ -235,54 +296,49 @@
         @pl.loop(0, number)
         def item(i):
             f, b = place(i)
-            part[1 + 2 * g, pl.ds(i, 1), :] = roll_window(f, b)
-
-        send(1 + 2 * g)
+            roll_window(f, b, lanes.at[1 + g, i])
+
+        if g == 0:
+            meet_plane()
+        gather_rows(g, 1 + 2 * g)
 
     def main_second(g):
-        slot = 1 + 2 * g
-        totals[slot] = receive(slot)
+        spread_rows(g, 1 + 2 * g)
         number, place = items(g)
 
         @pl.loop(0, number)
         def item(i):
             f, b = place(i)
-            center, scale = factors(total_row(slot, i), count_row(b))
-            part[slot + 1, pl.ds(i, 1), :] = clip_scores(f, b, center, scale)
-
-        send(slot + 1)
+            clip_scores(f, b, spread[g, i], lanes.at[1 + g, i])
+
+        gather_rows(g, 2 + 2 * g)
 
     def main_third(g):
-        slot = 1 + 2 * g
-        totals[slot + 1] = receive(slot + 1)
+        spread_rows(g, 2 + 2 * g)
         number, place = items(g)
 
         @pl.loop(0, number)
         def item(i):
             f, b = place(i)
-            count = count_row(b)
-            first = factors(total_row(slot, i), count)
-            second = factors(total_row(slot + 1, i), count)
-            finish(f, b, first, second, out.at[f], b * WINDOW)
+            finish(f, b, spread[g, i], out.at[f], b * WINDOW)
+
+    single = lanes.at[0, 0]
 
     def tail_first(f, b):
-        tail_part[2 * f] = roll_window(f, b)
+        roll_window(f, b, single)
+        tail_part[2 * f] = row_of(single[...])
         send_row(2 * f)
 
+    def tail_factors(slot, b):
+        return upright(factor_rows(receive_row(slot), totals[pl.ds(b, 1), :]))
+
     def tail_second(f, b):
-        slot = 2 * f
-        receive_row(slot)
-        center, scale = factors(tail_totals[slot], count_row(b))
-        tail_part[slot + 1] = clip_scores(f, b, center, scale)
-        send_row(slot + 1)
+        clip_scores(f, b, tail_factors(2 * f, b), single)
+        tail_part[2 * f + 1] = row_of(single[...])
+        send_row(2 * f + 1)
 
     def tail_third(f, b, target):
-        slot = 2 * f
-        receive_row(slot + 1)
-        count = count_row(b)
-        first = factors(tail_totals[slot], count)
-        second = factors(tail_totals[slot + 1], count)
-        finish(f, b, first, second, target, 0)
+        finish(f, b, tail_factors(2 * f + 1, b), target, 0)
 
     def ahead_first():
         upcoming.wait_recv()
@@ -297,8 +353,17 @@
 
     not_last = pl.when(jnp.logical_not(is_last))
 
+    def relay(copy):
+        def pass_on():
+            copy[0].wait_recv()
+            copy[1].start()
+
+        return pass_on
+
     def first(f):
         halos[f].wait_recv()
+        if f == ahead - 1:
+            pl.when(jnp.logical_not(is_first))(cross_onward.wait_recv)
         tail_first(f, 0)
 
     def second(f):
@@ -309,27 +374,35 @@
 
     main_first(0)
     main_first(1)
-    totals[0] = receive(0)
+    totals[...] = receive(0)
     main_second(0)
     not_last(ahead_first)
+    first(0)
     main_second(1)
-    first(0)
+    pl.when(is_last)(relay((even_detour, cross_onward)))
+    main_third(0)
     not_last(ahead_second)
-    main_third(0)
+    pl.when(tm == 1)(relay((even_detour, cross_onward)))
+    pl.when(is_last)(relay((odd_detour, back_onward)))
     second(0)
+    main_third(1)
+    first(1)
     not_last(ahead_third)
-    main_third(1)
     third(0)
-    for f in range(1, fields - 1):
-        first(f)
-        second(f)
-        third(f)
+    first(2)
+    second(1)
+    second(2)
+    third(1)
+    third(2)
 
     @pl.when(jnp.logical_not(is_first))
     def arrivals():
         finished.wait_recv()
         upcoming.wait_send()
 
+    pl.when(jnp.logical_not(is_last))(even_detour.wait_send)
+    pl.when(jnp.logical_not(is_even))(cross_onward.wait_send)
+    pl.when(is_last)(back_onward.wait_send)
     for copy in halos:
         copy.wait_send()
     for slot in range(part.shape[0]):
@@ -372,17 +445,23 @@
             vmem((1, assets), jnp.int32),
             vmem((1, assets), jnp.int32),
             vmem((WINDOW, assets), f32),
+            vmem((2, WINDOW, assets - DIRECT), f32),
+            vmem((1 + len(groups), stats, LANES, LANES), f32),
+            vmem((len(groups), stats, LANES, LANES), f32),
             vmem((slots, stats, LANES), f32),
             vmem((slots, n_as - 1, stats, LANES), f32),
-            vmem((slots, stats, LANES), f32),
+            vmem((stats, LANES), f32),
             vmem((2 * fields, 1, LANES), f32),
             vmem((2 * fields, n_as - 1, LANES), f32),
-            vmem((2 * fields, 1, LANES), f32),
             dma((fields + 2,)),
             dma((fields,)),
             dma((fields,)),
             dma((2,)),
             dma((2,)),
+            dma((1,)),
+            dma((2,)),
+            dma((2,)),
+            dma((1,)),
             pltpu.SemaphoreType.REGULAR,
             dma((slots,)),
             dma((slots,)),

time: 63.5 us -> 54.7 us (0.86)
  Pallas kernels: 59.9 us -> 51.1 us
    pallas_call x1, Pallas kernels: 59.9 us -> 51.1 us  [per_device(): pl.pallas_call(functools.partial(kernel, n_tm, n_as), out_shape=vmem((fie...]
where the time goes in v2:
time: 54.7 us; the launch traced here: 54.5 us
  Pallas kernels  51.1 us (93%)
  local copies, waits for them, and re-layouts  3.4 us (6%)
    pallas_call x1, Pallas kernels, per_device(): pl.pallas_call(functools.partial(kernel, n_tm, n_as), out_shape=vmem((fie...  51.1 us
    unnamed x1, local copies, waits for them, and re-layouts  3.4 us

profile of v2, /device:TPU:1, one launch (start us, length us, event | category | flops | bytes accessed | tf_op | source)
XLA Modules:
  0.0 54.5 jit_solution(5591919837199137043)
XLA Ops:
  0.0 51.1 %shard_map.37 = f32[4,256,2048]{2,1,0:T(8,128)S(1)} custom-call(f32[4,256,2048]{2,1,0:T(8,128)} %values.1, s32[1,2048]{1,0:T(1,128)} %bitcast.2, s32[1,2048]{1,0:T(1,128)} %bitcast.3), custom_call_target="tpu_custom_call" | custom-call | tf_op jit(solution)/shard_map/pallas_call | solution.py:435
  51.1 3.4 %copy.5 = f32[4,256,2048]{2,1,0:T(8,128)} copy(f32[4,256,2048]{2,1,0:T(8,128)S(1)} %shard_map.37) | data formatting | bytes 16777216

commit v3 on v2

--- a/solution.py
+++ b/solution.py
@@ -12,12 +12,25 @@
 CLIP = 3.0
 UNROLL = 4
 LINE = 8
-DIRECT = 1280
+DIRECT = 1024
+PIECES = 2
 
 
 def field_groups(fields):
     half = (fields + 1) // 2
     return [(start, min(half, fields - start)) for start in range(0, fields, half)]
+
+
+def plane(n_as, me):
+    lines, width = n_as // LINE, LINE // 2
+    steps = [(i, j, k) for i in range(lines) for j in range(width) for k in range(2)]
+    steps = [step for step in steps if step != (0, 0, 0)]
+    steps.sort(key=lambda s: -min(s[0], lines - s[0]) - min(s[1], width - s[1]))
+    row, column, core = lax.div(me, LINE), lax.rem(lax.div(me, 2), width), lax.rem(me, 2)
+    return [
+        lax.rem(row + i, lines) * LINE + lax.rem(column + j, width) * 2 + lax.rem(core + k, 2)
+        for i, j, k in steps
+    ]
 
 
 def kernel(
@@ -42,6 +55,7 @@
     spot = lax.rem(me, LINE)
     line_peers = [me - spot + lax.rem(spot + d, LINE) for d in range(1, LINE)]
     cross_peers = [lax.rem(me + LINE * d, n_as) for d in range(1, n_as // LINE)]
+    plane_peers = plane(n_as, me)
 
     dates = [
         pltpu.make_async_copy(opened_hbm, opened_ref, load_sem.at[fields]),
@@ -69,49 +83,28 @@
 
     @pl.when(is_first)
     def no_past():
-        x[ahead, :WINDOW, :] = jnp.zeros((WINDOW, assets), jnp.float32)
-        x[ahead - 1, :WINDOW, DIRECT:] = jnp.zeros((WINDOW, assets - DIRECT), jnp.float32)
+        for f in range(fields):
+            x[f, :WINDOW, :] = jnp.zeros((WINDOW, assets), jnp.float32)
 
     first_stamp = tm * rows - WINDOW
     for copy in dates:
         copy.wait()
 
-    @pl.loop(0, blocks + 2)
-    def listing(b):
-        start = pl.multiple_of(b * WINDOW, WINDOW)
-        stamps = first_stamp + start + lax.broadcasted_iota(jnp.int32, (WINDOW, LANES), 0)
-
-        def chunk(c, total):
-            cols = columns(c)
-            opened = jnp.maximum(opened_ref[:, cols], 0)
-            closed = closed_ref[:, cols]
-            listed = (stamps >= opened) & (stamps < closed)
-            low = jnp.maximum(stamps - (WINDOW - 1), opened)
-            counted = jnp.maximum(jnp.minimum(stamps + 1, closed) - low, 1).astype(jnp.float32)
-            ones = jnp.where(listed, 1.0, 0.0)
-            weight[pl.ds(start, WINDOW), cols] = ones
-            inverse[pl.ds(start, WINDOW), cols] = ones / counted
-            return total + ones
-
-        total = lax.fori_loop(0, chunks, chunk, zero, unroll=2)
-        here = lax.rem(b + blocks + 1, blocks + 2)
-        lanes[0, here, :WINDOW] = total
-        lanes[0, here, WINDOW:] = total
-
     pl.semaphore_wait(barrier, 3 + len(line_peers) + len(cross_peers))
 
     past = pl.ds(rows - WINDOW, WINDOW)
-    direct = [pl.ds(0, assets if f < ahead - 1 else DIRECT) for f in range(ahead)]
+    pieces = [(f, 0, assets) for f in range(ahead - 1)]
+    pieces += [(ahead - 1, start, DIRECT // PIECES) for start in range(0, DIRECT, DIRECT // PIECES)]
     rest = pl.ds(DIRECT, assets - DIRECT)
     halos = [
         pltpu.make_async_remote_copy(
-            src_ref=values.at[f, past, direct[f]],
-            dst_ref=x.at[f, pl.ds(0, WINDOW), direct[f]],
-            send_sem=halo_send.at[f],
-            recv_sem=halo_recv.at[f],
+            src_ref=values.at[f, past, pl.ds(start, width)],
+            dst_ref=x.at[f, pl.ds(0, WINDOW), pl.ds(start, width)],
+            send_sem=halo_send.at[k],
+            recv_sem=halo_recv.at[k],
             device_id={"tm": later},
         )
-        for f in range(fields - 1)
+        for k, (f, start, width) in enumerate(pieces)
     ]
     upcoming = pltpu.make_async_remote_copy(
         src_ref=values.at[ahead, pl.ds(0, WINDOW)],
@@ -154,18 +147,40 @@
     pl.when(is_even)(even_detour.start)
     pl.when(tm == 1)(odd_detour.start)
     for copy in halos:
-        copy.start()
+        pl.when(jnp.logical_not(is_last))(copy.start)
     for other in cross_peers:
         pl.semaphore_signal(ready, inc=1, device_id={"asset": other})
 
+    @pl.loop(0, blocks + 2)
+    def listing(b):
+        start = pl.multiple_of(b * WINDOW, WINDOW)
+        stamps = first_stamp + start + lax.broadcasted_iota(jnp.int32, (WINDOW, LANES), 0)
+
+        def chunk(c, total):
+            cols = columns(c)
+            opened = jnp.maximum(opened_ref[:, cols], 0)
+            closed = closed_ref[:, cols]
+            listed = (stamps >= opened) & (stamps < closed)
+            low = jnp.maximum(stamps - (WINDOW - 1), opened)
+            counted = jnp.maximum(jnp.minimum(stamps + 1, closed) - low, 1).astype(jnp.float32)
+            ones = jnp.where(listed, 1.0, 0.0)
+            weight[pl.ds(start, WINDOW), cols] = ones
+            inverse[pl.ds(start, WINDOW), cols] = ones / counted
+            return total + ones
+
+        total = lax.fori_loop(0, chunks, chunk, zero, unroll=2)
+        here = lax.rem(b + blocks + 1, blocks + 2)
+        lanes[0, here, :WINDOW] = total
+        lanes[0, here, WINDOW:] = total
+
     def send(slot):
-        for d in range(1, n_as):
+        for d, other in enumerate(plane_peers):
             pltpu.make_async_remote_copy(
                 src_ref=part.at[slot],
-                dst_ref=got.at[slot, d - 1],
+                dst_ref=got.at[slot, d],
                 send_sem=send_sem.at[slot],
                 recv_sem=recv_sem.at[slot],
-                device_id={"asset": lax.rem(me + d, n_as)},
+                device_id={"asset": other},
             ).start()
 
     def receive(slot):
@@ -174,13 +189,13 @@
         return part[slot] + jnp.sum(got[slot], axis=0)
 
     def send_row(slot):
-        for d in range(1, n_as):
+        for d, other in enumerate(plane_peers):
             pltpu.make_async_remote_copy(
                 src_ref=tail_part.at[slot],
-                dst_ref=tail_got.at[slot, pl.ds(d - 1, 1)],
+                dst_ref=tail_got.at[slot, pl.ds(d, 1)],
                 send_sem=tail_send.at[slot],
                 recv_sem=tail_recv.at[slot],
-                device_id={"asset": lax.rem(me + d, n_as)},
+                device_id={"asset": other},
             ).start()
 
     def receive_row(slot):
@@ -202,7 +217,7 @@
         return jnp.broadcast_to(row, (LANES, LANES)).T
 
 
-    def roll_window(f, b, place):
+    def roll_window(f, b, place, start=0, stop=chunks, begin=(zero, zero)):
         top = pl.multiple_of(b * WINDOW, WINDOW)
 
         def chunk(c, carry):
@@ -217,7 +232,7 @@
             rolling[f, pl.ds(top, WINDOW), cols] = means
             return carry[0] + means, carry[1] + means * means
 
-        total, square = lax.fori_loop(0, chunks, chunk, (zero, zero), unroll=UNROLL)
+        total, square = lax.fori_loop(start, stop, chunk, begin, unroll=UNROLL)
         place[:WINDOW] = total
         place[WINDOW:] = square
 
@@ -361,10 +376,16 @@
         return pass_on
 
     def first(f):
-        halos[f].wait_recv()
+        waits = [(halos[k].wait_recv, start, width) for k, (g, start, width) in enumerate(pieces) if g == f]
         if f == ahead - 1:
-            pl.when(jnp.logical_not(is_first))(cross_onward.wait_recv)
-        tail_first(f, 0)
+            waits.insert(0, (cross_onward.wait_recv, DIRECT, assets - DIRECT))
+        begin = (zero, zero)
+        for wait, start, width in waits:
+            pl.when(jnp.logical_not(is_first))(wait)
+            roll_window(f, 0, single, start // LANES, (start + width) // LANES, begin)
+            begin = (single[:WINDOW], single[WINDOW:])
+        tail_part[2 * f] = row_of(single[...])
+        send_row(2 * f)
 
     def second(f):
         tail_second(f, 0)
@@ -404,7 +425,7 @@
     pl.when(jnp.logical_not(is_even))(cross_onward.wait_send)
     pl.when(is_last)(back_onward.wait_send)
     for copy in halos:
-        copy.wait_send()
+        pl.when(jnp.logical_not(is_last))(copy.wait_send)
     for slot in range(part.shape[0]):
         sent = got.at[slot]
         pltpu.make_async_copy(sent, sent, send_sem.at[slot]).wait()
@@ -454,8 +475,8 @@
             vmem((2 * fields, 1, LANES), f32),
             vmem((2 * fields, n_as - 1, LANES), f32),
             dma((fields + 2,)),
-            dma((fields,)),
-            dma((fields,)),
+            dma((fields - 2 + PIECES,)),
+            dma((fields - 2 + PIECES,)),
             dma((2,)),
             dma((2,)),
             dma((1,)),

time: 54.7 us -> 50.5 us (0.923)
  the two profiles are of different devices: /device:TPU:1 before, /device:TPU:2 now
where the time goes in v3:
time: 50.5 us; the launch traced here: 50.4 us
  Pallas kernels  47 us (93%)
  local copies, waits for them, and re-layouts  3.4 us (7%)
    pallas_call x1, Pallas kernels, per_device(): pl.pallas_call(functools.partial(kernel, n_tm, n_as), out_shape=vmem((fie...  47 us
    unnamed x1, local copies, waits for them, and re-layouts  3.4 us

profile of v3, /device:TPU:2, one launch (start us, length us, event | category | flops | bytes accessed | tf_op | source)
XLA Modules:
  0.0 50.4 jit_solution(9463521558014278017)
XLA Ops:
  0.0 47.0 %shard_map.37 = f32[4,256,2048]{2,1,0:T(8,128)S(1)} custom-call(f32[4,256,2048]{2,1,0:T(8,128)} %values.1, s32[1,2048]{1,0:T(1,128)} %bitcast.2, s32[1,2048]{1,0:T(1,128)} %bitcast.3), custom_call_target="tpu_custom_call" | custom-call | tf_op jit(solution)/shard_map/pallas_call | solution.py:456
  47.0 3.4 %copy.5 = f32[4,256,2048]{2,1,0:T(8,128)} copy(f32[4,256,2048]{2,1,0:T(8,128)S(1)} %shard_map.37) | data formatting | bytes 16777216

commit v4 on v3

--- a/solution.py
+++ b/solution.py
@@ -12,8 +12,9 @@
 CLIP = 3.0
 UNROLL = 4
 LINE = 8
-DIRECT = 1024
-PIECES = 2
+DIRECT = 896
+PIECES = 7
+RELAYS = 3
 
 
 def field_groups(fields):
@@ -95,7 +96,8 @@
     past = pl.ds(rows - WINDOW, WINDOW)
     pieces = [(f, 0, assets) for f in range(ahead - 1)]
     pieces += [(ahead - 1, start, DIRECT // PIECES) for start in range(0, DIRECT, DIRECT // PIECES)]
-    rest = pl.ds(DIRECT, assets - DIRECT)
+    share = (assets - DIRECT) // RELAYS
+    rest = [pl.ds(DIRECT + k * share, share) for k in range(RELAYS)]
     halos = [
         pltpu.make_async_remote_copy(
             src_ref=values.at[f, past, pl.ds(start, width)],
@@ -122,30 +124,37 @@
     )
 
     def detour(slot, other):
-        return pltpu.make_async_remote_copy(
-            src_ref=values.at[ahead - 1, past, rest],
-            dst_ref=hold.at[slot],
-            send_sem=hold_send.at[0],
-            recv_sem=hold_recv.at[slot],
-            device_id={"tm": other},
-        )
+        return [
+            pltpu.make_async_remote_copy(
+                src_ref=values.at[ahead - 1, past, rest[k]],
+                dst_ref=hold.at[slot, k],
+                send_sem=hold_send.at[k],
+                recv_sem=hold_recv.at[slot, k],
+                device_id={"tm": other},
+            )
+            for k in range(RELAYS)
+        ]
 
     def onward(slot, other):
-        return pltpu.make_async_remote_copy(
-            src_ref=hold.at[slot],
-            dst_ref=x.at[ahead - 1, pl.ds(0, WINDOW), rest],
-            send_sem=late_send.at[slot],
-            recv_sem=late_recv.at[0],
-            device_id={"tm": other},
-        )
+        return [
+            pltpu.make_async_remote_copy(
+                src_ref=hold.at[slot, k],
+                dst_ref=x.at[ahead - 1, pl.ds(0, WINDOW), rest[k]],
+                send_sem=late_send.at[slot, k],
+                recv_sem=late_recv.at[k],
+                device_id={"tm": other},
+            )
+            for k in range(RELAYS)
+        ]
 
     is_even = lax.rem(tm, 2) == 0
     even_detour, odd_detour = detour(0, before), detour(1, across)
     cross_onward, back_onward = onward(0, across), onward(1, before)
 
     pl.when(jnp.logical_not(is_first))(upcoming.start)
-    pl.when(is_even)(even_detour.start)
-    pl.when(tm == 1)(odd_detour.start)
+    for k in range(RELAYS):
+        pl.when(is_even)(even_detour[k].start)
+        pl.when(tm == 1)(odd_detour[k].start)
     for copy in halos:
         pl.when(jnp.logical_not(is_last))(copy.start)
     for other in cross_peers:
@@ -368,17 +377,19 @@
 
     not_last = pl.when(jnp.logical_not(is_last))
 
-    def relay(copy):
+    def relay(arriving, leaving, k):
         def pass_on():
-            copy[0].wait_recv()
-            copy[1].start()
+            arriving[k].wait_recv()
+            leaving[k].start()
 
         return pass_on
 
     def first(f):
         waits = [(halos[k].wait_recv, start, width) for k, (g, start, width) in enumerate(pieces) if g == f]
         if f == ahead - 1:
-            waits.insert(0, (cross_onward.wait_recv, DIRECT, assets - DIRECT))
+            waits += [
+                (cross_onward[k].wait_recv, DIRECT + k * share, share) for k in range(RELAYS)
+            ]
         begin = (zero, zero)
         for wait, start, width in waits:
             pl.when(jnp.logical_not(is_first))(wait)
@@ -399,18 +410,24 @@
     main_second(0)
     not_last(ahead_first)
     first(0)
+    pl.when(is_last)(relay(even_detour, cross_onward, 0))
     main_second(1)
-    pl.when(is_last)(relay((even_detour, cross_onward)))
+    pl.when(is_last)(relay(even_detour, cross_onward, 1))
     main_third(0)
+    pl.when(is_last)(relay(even_detour, cross_onward, 2))
     not_last(ahead_second)
-    pl.when(tm == 1)(relay((even_detour, cross_onward)))
-    pl.when(is_last)(relay((odd_detour, back_onward)))
+    pl.when(tm == 1)(relay(even_detour, cross_onward, 0))
+    pl.when(is_last)(relay(odd_detour, back_onward, 0))
+    pl.when(is_last)(relay(odd_detour, back_onward, 1))
     second(0)
+    pl.when(tm == 1)(relay(even_detour, cross_onward, 1))
+    pl.when(is_last)(relay(odd_detour, back_onward, 2))
     main_third(1)
+    pl.when(tm == 1)(relay(even_detour, cross_onward, 2))
+    not_last(ahead_third)
     first(1)
-    not_last(ahead_third)
+    first(2)
     third(0)
-    first(2)
     second(1)
     second(2)
     third(1)
@@ -421,9 +438,10 @@
         finished.wait_recv()
         upcoming.wait_send()
 
-    pl.when(jnp.logical_not(is_last))(even_detour.wait_send)
-    pl.when(jnp.logical_not(is_even))(cross_onward.wait_send)
-    pl.when(is_last)(back_onward.wait_send)
+    for k in range(RELAYS):
+        pl.when(jnp.logical_not(is_last))(even_detour[k].wait_send)
+        pl.when(jnp.logical_not(is_even))(cross_onward[k].wait_send)
+        pl.when(is_last)(back_onward[k].wait_send)
     for copy in halos:
         pl.when(jnp.logical_not(is_last))(copy.wait_send)
     for slot in range(part.shape[0]):
@@ -466,7 +484,7 @@
             vmem((1, assets), jnp.int32),
             vmem((1, assets), jnp.int32),
             vmem((WINDOW, assets), f32),
-            vmem((2, WINDOW, assets - DIRECT), f32),
+            vmem((2, RELAYS, WINDOW, (assets - DIRECT) // RELAYS), f32),
             vmem((1 + len(groups), stats, LANES, LANES), f32),
             vmem((len(groups), stats, LANES, LANES), f32),
             vmem((slots, stats, LANES), f32),
@@ -479,10 +497,10 @@
             dma((fields - 2 + PIECES,)),
             dma((2,)),
             dma((2,)),
-            dma((1,)),
-            dma((2,)),
-            dma((2,)),
-            dma((1,)),
+            dma((RELAYS,)),
+            dma((2, RELAYS)),
+            dma((2, RELAYS)),
+            dma((RELAYS,)),
             pltpu.SemaphoreType.REGULAR,
             dma((slots,)),
             dma((slots,)),

time: 50.5 us -> 50.3 us (level)
  no operation moved by 1% of the time
where the time goes in v4:
time: 50.3 us; the launch traced here: 50.2 us
  Pallas kernels  46.8 us (93%)
  local copies, waits for them, and re-layouts  3.4 us (7%)
    pallas_call x1, Pallas kernels, per_device(): pl.pallas_call(functools.partial(kernel, n_tm, n_as), out_shape=vmem((fie...  46.8 us
    unnamed x1, local copies, waits for them, and re-layouts  3.4 us

profile of v4, /device:TPU:2, one launch (start us, length us, event | category | flops | bytes accessed | tf_op | source)
XLA Modules:
  0.0 50.2 jit_solution(15487442001460792464)
XLA Ops:
  0.0 46.8 %shard_map.37 = f32[4,256,2048]{2,1,0:T(8,128)S(1)} custom-call(f32[4,256,2048]{2,1,0:T(8,128)} %values.1, s32[1,2048]{1,0:T(1,128)} %bitcast.2, s32[1,2048]{1,0:T(1,128)} %bitcast.3), custom_call_target="tpu_custom_call" | custom-call | tf_op jit(solution)/shard_map/pallas_call | solution.py:474
  46.8 3.4 %copy.5 = f32[4,256,2048]{2,1,0:T(8,128)} copy(f32[4,256,2048]{2,1,0:T(8,128)S(1)} %shard_map.37) | data formatting | bytes 16777216
